TPU v7x, 32 devices: a whole 2x2x4 slice. The times are simulated.
32 devices in a mesh: dp: 4 (over y, core), tp: 8 (over z, x).
Axes of the slice: x: 2, y: 2, z: 4, core: 2. Of those that a mesh axis runs over, the one named last changes fastest.
Arguments:
- tokens: bfloat16 [2560, 6144], P(('dp', 'tp')), parts along dimension 0, may hold values from -6 to 6
- ln_gain: float32 [6144], replicated, may hold values from 0.25 to 1.75
- ln_bias: float32 [6144], replicated, may hold values from -1.75 to 1.75
- w_qkv: bfloat16 [6144, 3, 6144], P(None, None, 'tp'), may hold values from -0.45927933 to 0.45927933
- b_qkv: float32 [3, 6144], P(None, 'tp'), may hold values from -3 to 3
- w_out: bfloat16 [6144, 6144], P('tp'), may hold values from -0.078125 to 0.078125
- b_out: float32 [6144], replicated, may hold values from -1.25 to 1.25
- kv_cache: bfloat16 [2, 28, 128, 6144], P(None, 'dp', None, 'tp'), parts along dimension 1, may hold values from -6 to 6
- page_table: int32 [4, 5], P('dp'), parts along dimension 0, may hold values from 0 to 6, as said below
- lengths: int32 [4], P('dp'), parts along dimension 0, may hold values from 321 to 640
Outputs:
- attn_out: bfloat16 [2560, 6144], P(('dp', 'tp')), parts along dimension 0
- kv_cache_out: bfloat16 [2, 28, 128, 6144], P(None, 'dp', None, 'tp'), parts along dimension 1
There are 4 independent parts, one for each index of `dp`. A program takes and returns all parts, laid end to end along the dimension named above; an argument that names none is the same for every part. Nothing has to cross between parts.
Inputs may be any that keep to these rules, and one draw needn't show every extreme that they name: `page_table`: no slot is named twice within a part.
All inputs are finite; a program needn't handle non-finite values.
Results may differ from a plain program's by a relative error of at most 0.015.
The roundings to bfloat16 on the way count: a program that leaves them out, or rounds other values in their place, can miss the bound.
Values may be sent and summed in bfloat16 or wider, within the bound.
A program may use at most 128 MiB of HBM per device.

v0:
```python
import math

import jax
import jax.numpy as jnp
from jax import lax
from jax.sharding import PartitionSpec as P

HD = 128
SEQS = 1


norm_eps = 1e-05


def layer_norm(token_rows, gain_row, shift_row):
    floats = token_rows.astype(jnp.float32)
    center = jnp.mean(floats, axis=-1, keepdims=True)
    spread = jnp.mean(jnp.square(floats - center), axis=-1, keepdims=True)
    return ((floats - center) * lax.rsqrt(spread + norm_eps) * gain_row + shift_row).astype(
        jnp.bfloat16
    )


def attend(queries, keys, values, lengths):
    seq_count, seq_len, head_count, head_dim = queries.shape
    block_len = math.gcd(seq_len, 512)
    score_scale = 1.0 / math.sqrt(head_dim)
    key_pos = jnp.arange(seq_len, dtype=jnp.int32)

    def one_sequence(inputs):
        seq_query, seq_key, seq_value, length = inputs
        blocks = seq_query.reshape(seq_len // block_len, block_len, head_count, head_dim)

        def one_block(block_pair):
            block_query, block_index = block_pair
            scores = (
                jnp.einsum("qhe,khe->hqk", block_query, seq_key, preferred_element_type=jnp.float32)
                * score_scale
            )
            query_pos = block_index * block_len + jnp.arange(block_len, dtype=jnp.int32)
            allowed = (key_pos[None, :] <= query_pos[:, None]) & (key_pos[None, :] < length)
            scores = jnp.where(allowed[None], scores, -1e30)
            row_max = jnp.max(scores, axis=-1, keepdims=True)
            raised = jnp.exp(scores - row_max)
            weights = (raised / jnp.sum(raised, axis=-1, keepdims=True)).astype(jnp.bfloat16)
            return jnp.einsum(
                "hqk,khe->qhe", weights, seq_value, preferred_element_type=jnp.float32
            ).astype(jnp.bfloat16)

        results = lax.map(one_block, (blocks, jnp.arange(seq_len // block_len, dtype=jnp.int32)))
        return results.reshape(seq_len, head_count, head_dim)

    return lax.map(one_sequence, (queries, keys, values, lengths))


def write_cache(kv_cache, key_value, page_table, lengths):
    seq_count, page_count = page_table.shape
    page_len = kv_cache.shape[2]
    feat_here = kv_cache.shape[3]
    fresh_pages = jnp.moveaxis(key_value, 1, 0).reshape(
        2, seq_count * page_count, page_len, feat_here
    )
    slot_ids = page_table.reshape(-1)
    positions = (
        jnp.arange(page_count, dtype=jnp.int32)[:, None] * page_len
        + jnp.arange(page_len, dtype=jnp.int32)[None, :]
    )
    written = (positions[None] < lengths[:, None, None]).reshape(seq_count * page_count, page_len)
    current = kv_cache[:, slot_ids]
    new_pages = jnp.where(written[None, :, :, None], fresh_pages, current)
    return kv_cache.at[:, slot_ids].set(new_pages)


def body(tokens, ln_gain, ln_bias, w_qkv, b_qkv, w_out, b_out, kv_cache, page_table, lengths):
    model_width = tokens.shape[1]
    local_feat = w_qkv.shape[2]
    weights_flat = w_qkv.reshape(model_width, 3 * local_feat)
    bias_flat = b_qkv.reshape(-1)
    normed = layer_norm(tokens, ln_gain, ln_bias)
    block_rows = lax.all_gather(normed, "tp", axis=0, tiled=True)
    result = jnp.dot(block_rows, weights_flat, preferred_element_type=jnp.float32) + bias_flat
    projected = result.astype(jnp.bfloat16).reshape(block_rows.shape[0], 3, local_feat)
    all_rows = projected.shape[0]
    seq_len = all_rows // SEQS
    heads_here = local_feat // HD
    queries = projected[:, 0].reshape(SEQS, seq_len, heads_here, HD)
    keys = projected[:, 1].reshape(SEQS, seq_len, heads_here, HD)
    values = projected[:, 2].reshape(SEQS, seq_len, heads_here, HD)
    attended = attend(queries, keys, values, lengths).reshape(all_rows, local_feat)
    summed = lax.psum_scatter(
        jnp.dot(attended, w_out, preferred_element_type=jnp.float32).astype(jnp.bfloat16),
        "tp",
        scatter_dimension=0,
        tiled=True,
    ).astype(jnp.float32)
    attn_out = (summed + b_out).astype(jnp.bfloat16)
    kv_cache_out = write_cache(kv_cache, projected[:, 1:3], page_table, lengths)
    return (attn_out, kv_cache_out)


def solution(mesh):
    placed = (
        P(("dp", "tp"), None),
        P(),
        P(),
        P(None, None, "tp"),
        P(None, "tp"),
        P("tp", None),
        P(),
        P(None, "dp", None, "tp"),
        P("dp", None),
        P("dp"),
    )
    return jax.shard_map(
        body,
        mesh=mesh,
        in_specs=placed,
        out_specs=(P(("dp", "tp"), None), P(None, "dp", None, "tp")),
        check_vma=False,
    )
```

profile of v0, /device:TPU:0, one launch (start us, length us, event | category | flops | bytes accessed | tf_op | source)
XLA Modules:
  0.0 379.3 jit_solution(2735044631547351451)
XLA Ops:
  7.2 3.6 copy.49
  11.6 1.4 fusion.29
  13.0 36.9 %copy.21 = bf16[6144,3,768]{0,2,1:T(8,128)(2,1)} copy(bf16[6144,3,768]{2,0,1:T(8,128)(2,1)} %param.15) | data formatting | bytes 56623104 | tf_op args[3]
  49.9 83.8 %all-gather.2.cloned.1.call-done = bf16[640,6144]{1,0:T(8,128)(2,1)} async-done(((bf16[80,6144]{1,0:T(8,128)(2,1)}), bf16[640,6144]{1,0:T(8,128)(2,1)}) %all-gather.2.cloned.1.call-update) | async-done | bytes 7864336 | tf_op jit(solution)/shard_map/all_gather | solution.py:80
  133.8 25.8 %add_convert_fusion = bf16[640,2304]{1,0:T(8,128)(2,1)} fusion(bf16[640,6144]{1,0:T(8,128)(2,1)} %all-gather.2.cloned.1.call-done, bf16[6144,2304]{0,1:T(8,128)(2,1)} %bitcast.59, f32[2304]{0:T(1024)S(1)} %add.87), kind=kOutput, calls=%fused_computation.26 | convolution fusion | flops 18122342400 | bytes 39134208 | tf_op jit(solution)/shard_map/dot_general | solution.py:81
  159.6 4.1 %copy.22 = bf16[640,2304]{0,1:T(8,128)(2,1)S(1)} copy(bf16[640,2304]{1,0:T(8,128)(2,1)} %add_convert_fusion) | data formatting | bytes 5898240 | tf_op jit(solution)/shard_map/convert_element_type | solution.py:82
  163.7 1.7 fusion.37
  165.4 3.5 reshape.187
  168.9 2.6 copy.24
  171.5 2.2 copy.25
  173.7 2.2 copy.26
  175.9 41.7 %while.19 = (s32[]{:T(128)}, bf16[5,128,6,128]{3,1,2,0:T(8,128)(2,1)}, s32[5]{0:T(128)S(1)}, s32[]{:T(128)}, bf16[5,128,6,128]{3,1,2,0:T(8,128)(2,1)}, /*index=5...) while((s32[]{:T(128)}, ...), condition=%wide.region_5.6_spmd.clone.clone, body=%wide.region_2.5_spmd.clone.clone.sunk | while | flops 254870912 | bytes 6464893 | solution.py:50
  177.1 0.7 iota_compare_fusion.3
  177.9 3.5 fusion.53
  181.3 2.9 fusion.54
  186.2 3.5 fusion.53
  189.7 2.9 fusion.54
  194.6 3.5 fusion.53
  198.0 2.9 fusion.54
  202.9 3.5 fusion.53
  206.4 2.9 fusion.54
  211.2 3.5 fusion.53
  214.7 2.9 fusion.54
  217.6 1.9 copy.27
  219.5 12.1 %convolution_convert_fusion.1 = bf16[640,6144]{1,0:T(8,128)(2,1)} fusion(bf16[768,6144]{1,0:T(8,128)(2,1)} %param.17, bf16[80,8,6,128]{3,2,1,0:T(8,128)(2,1)S(1)} %bitcast.65), kind=kOutput, calls=%fused_computation.25 | convolution fusion | flops 6043729920 | bytes 18284544 | tf_op jit(solution)/shard_map/dot_general | solution.py:91
  232.3 3.9 %gather_fusion = bf16[5,2,128,768]{3,2,1,0:T(8,128)(2,1)} fusion(bf16[2,7,128,768]{3,2,1,0:T(8,128)(2,1)} %copy.49, s32[1024]{0:T(1024)S(1)} %pad_clamp_fusion), kind=kCustom, calls=%fused_computation | custom fusion | bytes 3932180 | tf_op jit(solution)/shard_map/gather | solution.py:69
  236.3 1.6 slice_bitcast_fusion
  237.9 4.1 %copy.28 = bf16[2,640,768]{2,1,0:T(8,128)(2,1)} copy(bf16[2,640,768]{1,2,0:T(8,128)(2,1)} %slice_bitcast_fusion) | data formatting | bytes 3932160 | tf_op jit(solution)/shard_map/transpose | solution.py:60
  241.9 3.9 %fusion.30 = bf16[5,2,128,768]{3,2,1,0:T(8,128)(2,1)} fusion(bf16[5,2,128,768]{3,2,1,0:T(8,128)(2,1)} %gather_fusion, bf16[2,5,128,768]{3,2,1,0:T(8,128)(2,1)} %bitcast.62, pred[5,128]{1,0:T(8,128)(4,1)S(1)} %add_compare_fusion), kind=kLoop, calls=%fused_computation.37 | loop fusion | flops 983040 | bytes 5898880 | tf_op jit(solution)/shard_map/jit(_where)/select_n | solution.py:70
  245.8 4.2 %scatter_fusion = bf16[2,7,128,768]{3,2,1,0:T(8,128)(2,1)S(1)} fusion(bf16[2,7,128,768]{3,2,1,0:T(8,128)(2,1)S(1)} %copy-done, s32[5]{0:T(128)S(1)} %fusion.33, bf16[5,2,128,768]{3,2,1,0:T(8,128)(2,1)} %fusion.30), kind=kCustom, calls=%fused_computation.1 | custom fusion | bytes 5898260 | tf_op jit(solution)/shard_map/scatter | solution.py:71
  250.0 120.1 %reduce-scatter.2.cloned.1.call-done = bf16[80,6144]{1,0:T(8,128)(2,1)} async-done(((bf16[640,6144]{1,0:T(8,128)(2,1)}), bf16[80,6144]{1,0:T(8,128)(2,1)}) %reduce-scatter.2.cloned.1.call-update) | async-done | bytes 983056 | tf_op jit(solution)/shard_map/reduce_scatter | solution.py:90
  370.2 2.3 add_convert_fusion.1
  (50 shorter events, 7.1 us)
Async XLA Ops:
  7.2 3.6 copy-start.2
  7.2 126.6 %all-gather.2.cloned.1.call-start = ((), (), s32[]{:S(2)}) async-start(), calls=%async_computation.1 | async-start | bytes 8847360 | tf_op jit(solution)/shard_map/all_gather | solution.py:80
  10.8 0.7 copy-start.3
  10.8 0.8 copy-start.4
  13.0 357.2 %reduce-scatter.2.cloned.1.call-start = ((), (), s32[]{:S(2)}) async-start(), calls=%async_computation.2 | async-start | bytes 8847360 | tf_op jit(solution)/shard_map/reduce_scatter | solution.py:90
  13.0 36.9 %copy-start.6 = (f32[3,768]{1,0:T(4,128)S(1)}, f32[3,768]{1,0:T(4,128)}, u32[]{:S(2)}) copy-start(f32[3,768]{1,0:T(4,128)} %param.16) | copy-start | bytes 27652
  231.6 0.7 copy-start.7
  241.9 3.9 %copy-start = (bf16[2,7,128,768]{3,2,1,0:T(8,128)(2,1)S(1)}, bf16[2,7,128,768]{3,2,1,0:T(8,128)(2,1)}, u32[]{:S(2)}) copy-start(bf16[2,7,128,768]{3,2,1,0:T(8,128)(2,1)} %copy.49) | copy-start | bytes 8257540
  245.8 124.3 %copy-start.5 = (f32[6144]{0:T(1024)S(1)}, f32[6144]{0:T(1024)}, u32[]{:S(2)}) copy-start(f32[6144]{0:T(1024)} %param.18) | copy-start | bytes 73732
  250.0 122.5 %copy-start.1 = (bf16[2,7,128,768]{3,2,1,0:T(8,128)(2,1)}, bf16[2,7,128,768]{3,2,1,0:T(8,128)(2,1)S(1)}, u32[]{:S(2)}) copy-start(bf16[2,7,128,768]{3,2,1,0:T(8,128)(2,1)S(1)} %scatter_fusion) | copy-start | bytes 8257540
Sparse Core Ops, SparseCore 0:
  13.1 120.6 all-gather.1
  231.7 138.3 reduce-scatter.1
where the time goes:
time: 381 us; the launch traced here: 379 us
  waiting for transfers between devices  204 us (54%)
  local copies, waits for them, and re-layouts  75.4 us (20%)
  matrix products  69.8 us (18%)
  between operations  14.8 us (4%)
  other arithmetic  12.3 us (3%)
    reduce_scatter x1, waiting for transfers between devices, body(): lax.psum_scatter(jnp.dot(attended, w_out, preferred_element_type=jnp.floa...  120 us
    all_gather x1, waiting for transfers between devices, body(): block_rows = lax.all_gather(normed, 'tp', axis=0, tiled=True)  83.8 us
    unnamed x21, local copies, waits for them, and re-layouts  47.6 us
    dot_general x1, matrix products, body(): jnp.dot(block_rows, weights_flat, preferred_element_type=jnp.float32)  25.8 us
    sub x5, matrix products, one_block(): raised = jnp.exp(scores - row_max)  17.3 us
    dot_general x5, matrix products, one_block(): jnp.einsum('hqk,khe->qhe', weights, seq_value, preferred_element_type=jnp...  14.7 us
    dot_general x1, matrix products, body(): jnp.dot(attended, w_out, preferred_element_type=jnp.float32)  12.1 us
  transfers between devices with their start and end apart: 2, of which 2 were waited for; matrix products, arithmetic and copies ran while one was open for 14% of the time, Pallas kernels for 0%

commit v1 on v0

v1 whole, which is shorter than its diff:
```python
import functools
import math

import jax
import jax.numpy as jnp
import numpy as np
from jax import lax
from jax.experimental import pallas as pl
from jax.experimental.pallas import tpu as pltpu
from jax.sharding import PartitionSpec as P

HD = 128
CHUNKS = 4
MESH = pl.DeviceIdType.MESH

norm_eps = 1e-05


def layer_norm(token_rows, gain_row, shift_row):
    floats = token_rows.astype(jnp.float32)
    center = jnp.mean(floats, axis=-1, keepdims=True)
    spread = jnp.mean(jnp.square(floats - center), axis=-1, keepdims=True)
    return ((floats - center) * lax.rsqrt(spread + norm_eps) * gain_row + shift_row).astype(
        jnp.bfloat16
    )


def ring_order(mesh):
    n = mesh.shape["tp"]
    line = np.moveaxis(mesh.devices, mesh.axis_names.index("tp"), -1).reshape(-1, n)[0]
    coords = [tuple(getattr(d, "coords", None) or ()) for d in line]
    wide = len({c[0] for c in coords if c})
    if wide < 2 or n % wide or (n // wide) % 2:
        return list(range(n))
    tall = n // wide
    order = [0]
    for z in range(tall):
        xs = range(1, wide) if z % 2 == 0 else range(wide - 1, 0, -1)
        order += [z * wide + x for x in xs]
    order += [z * wide for z in range(tall - 1, 0, -1)]
    return order


def pick(table, index):
    value = jnp.int32(0)
    for k, entry in enumerate(table):
        value = value + jnp.where(index == k, entry, 0)
    return value


def fused(order, x_ref, w_hbm, b_ref, wo_hbm, bo_ref, len_ref, out_ref, kv_hbm,
          xg, w_v, wo_v, proj, att, first, rs,
          ag_send, ag_recv, rs_send, rs_recv, w_sem, wo_sem, kv_sem):
    n = len(order)
    h = n // 2
    rows, model = x_ref.shape
    mid = model // 2
    feat = w_v.shape[2]
    total = proj.shape[1]
    me = lax.axis_index("tp")
    inverse = [order.index(i) for i in range(n)]
    place = pick(inverse, me)

    def at(offset):
        return pick(order, lax.rem(place + offset + n, n))

    peers = (at(1), at(-1))
    for c in range(3):
        pltpu.make_async_copy(w_hbm.at[c], w_v.at[c], w_sem.at[c]).start()

    barrier = pltpu.get_barrier_semaphore()
    for peer in peers:
        pl.semaphore_signal(barrier, inc=1, device_id={"tp": peer}, device_id_type=MESH)
    pl.semaphore_wait(barrier, 2)

    def slot(way, s):
        return n - 1 if s == h else 2 * s - 1 + way

    def gather(way, s, half):
        dst = xg.at[half, pl.ds(slot(way, s) * rows, rows)]
        if s == 1:
            src = x_ref.at[:, pl.ds(half * mid, mid)]
        else:
            src = xg.at[half, pl.ds(slot(way, s - 1) * rows, rows)]
        return pltpu.make_async_remote_copy(
            src_ref=src, dst_ref=dst,
            send_sem=ag_send.at[way, s, half], recv_sem=ag_recv.at[way, s, half],
            device_id={"tp": peers[way]}, device_id_type=MESH)

    gathers = [(way, s, half) for s in range(1, h + 1) for half in range(2) for way in range(2)
               if s < h or way == half]
    for g in gathers:
        if g[1] == 1:
            gather(*g).start()
    wo_copy = pltpu.make_async_copy(wo_hbm, wo_v, wo_sem)
    wo_copy.start()
    for c in range(3):
        pltpu.make_async_copy(w_hbm.at[c], w_v.at[c], w_sem.at[c]).wait()

    tn = math.gcd(feat, 256)

    def project(lhs, owners):
        @pl.loop(0, 3)
        def _(c):
            @pl.loop(0, feat // tn)
            def _(j):
                cols = pl.ds(pl.multiple_of(j * tn, tn), tn)
                acc = jnp.dot(lhs(0), w_v[c, pl.ds(0, mid), cols],
                              preferred_element_type=jnp.float32)
                acc += jnp.dot(lhs(1), w_v[c, pl.ds(mid, mid), cols],
                               preferred_element_type=jnp.float32)
                done = (acc + b_ref[c, :, cols]).astype(jnp.bfloat16)
                for i, owner in enumerate(owners):
                    dst = pl.ds(pl.multiple_of(owner * rows, rows), rows)
                    proj[c, dst, cols] = done[i * rows:(i + 1) * rows]

    project(lambda half: x_ref[:, pl.ds(half * mid, mid)], [me])
    for s in range(1, h + 1):
        for half in range(2):
            for way in range(2):
                if (way, s, half) in gathers:
                    gather(way, s, half).wait_recv()
                    if (way, s + 1, half) in gathers:
                        gather(way, s + 1, half).start()
        if s < h:
            project(lambda half: xg[half, pl.ds((2 * s - 1) * rows, 2 * rows)], [at(-s), at(s)])
        else:
            project(lambda half: xg[half, pl.ds((n - 1) * rows, rows)], [at(h)])
    kv_copy = pltpu.make_async_copy(proj.at[pl.ds(1, 2)], kv_hbm, kv_sem)
    kv_copy.start()

    scale = 1.0 / math.sqrt(HD)
    length = len_ref[0]

    def attend(owners):
        key_pos = lax.broadcasted_iota(jnp.int32, (rows, total), 1)
        row_pos = lax.broadcasted_iota(jnp.int32, (rows, total), 0)

        @pl.loop(0, feat // HD)
        def _(head):
            cols = pl.ds(pl.multiple_of(head * HD, HD), HD)
            key, value = proj[1, :, cols], proj[2, :, cols]
            for i, owner in enumerate(owners):
                query = proj[0, pl.ds(pl.multiple_of(owner * rows, rows), rows), cols]
                scores = lax.dot_general(query, key, (((1,), (1,)), ((), ())),
                                         preferred_element_type=jnp.float32) * scale
                allowed = (key_pos <= row_pos + owner * rows) & (key_pos < length)
                scores = jnp.where(allowed, scores, -1e30)
                raised = jnp.exp(scores - jnp.max(scores, axis=-1, keepdims=True))
                weights = (raised / jnp.sum(raised, axis=-1, keepdims=True)).astype(jnp.bfloat16)
                att[pl.ds(i * rows, rows), cols] = jnp.dot(
                    weights, value, preferred_element_type=jnp.float32).astype(jnp.bfloat16)

    chunk = model // CHUNKS
    to = math.gcd(chunk, 512)

    def scatter(way, d, q):
        cols = pl.ds(q * chunk, chunk)
        src = first.at[:, cols] if d == h else rs.at[way, d, :, cols]
        return pltpu.make_async_remote_copy(
            src_ref=src, dst_ref=rs.at[way, d - 1, :, cols],
            send_sem=rs_send.at[way, d, q], recv_sem=rs_recv.at[way, d, q],
            device_id={"tp": peers[way]}, device_id_type=MESH)

    scatters = [(way, d, q) for d in range(h, 0, -1) for q in range(CHUNKS) for way in range(2)
                if d < h or way == q // (CHUNKS // 2)]

    wo_copy.wait()
    attend([at(h)])
    for q in range(CHUNKS):
        @pl.loop(0, chunk // to)
        def _(j):
            cols = pl.ds(pl.multiple_of(q * chunk + j * to, to), to)
            first[:, cols] = jnp.dot(att[pl.ds(0, rows), :], wo_v[:, cols],
                                     preferred_element_type=jnp.float32).astype(jnp.bfloat16)
        for way in range(2):
            if (way, h, q) in scatters:
                scatter(way, h, q).start()

    for d in range(h - 1, 0, -1):
        attend([at(d), at(-d)])
        half = CHUNKS // 2
        for q in ([0, half] + [c for c in range(CHUNKS) if c not in (0, half)]):
            have = [(way, d + 1, q) in scatters for way in range(2)]
            for way in range(2):
                if have[way]:
                    scatter(way, d + 1, q).wait_recv()

            @pl.loop(0, chunk // to)
            def _(j):
                cols = pl.ds(pl.multiple_of(q * chunk + j * to, to), to)
                part = jnp.dot(att[...], wo_v[:, cols], preferred_element_type=jnp.float32)
                for way in range(2):
                    mine = part[way * rows:(way + 1) * rows]
                    if have[way]:
                        mine = mine + rs[way, d, :, cols].astype(jnp.float32)
                    rs[way, d, :, cols] = mine.astype(jnp.bfloat16)
            for way in range(2):
                scatter(way, d, q).start()

    attend([me])
    half = CHUNKS // 2
    for q in ([0, half] + [c for c in range(CHUNKS) if c not in (0, half)]):
        for way in range(2):
            scatter(way, 1, q).wait_recv()

        @pl.loop(0, chunk // to)
        def _(j):
            cols = pl.ds(pl.multiple_of(q * chunk + j * to, to), to)
            part = jnp.dot(att[pl.ds(0, rows), :], wo_v[:, cols],
                           preferred_element_type=jnp.float32)
            part += rs[0, 0, :, cols].astype(jnp.float32) + rs[1, 0, :, cols].astype(jnp.float32)
            out_ref[:, cols] = (part + bo_ref[:, cols]).astype(jnp.bfloat16)

    for g in gathers:
        gather(*g).wait_send()
    for g in scatters:
        scatter(*g).wait_send()
    kv_copy.wait()


def fill_page(pages_ref, length_ref, cache_ref, fresh_ref, out_ref):
    page = pages_ref[pl.program_id(0)]
    page_len = out_ref.shape[2]
    left = jnp.where(page >= 0, length_ref[0] - page * page_len, 0)
    pos = lax.broadcasted_iota(jnp.int32, (2, 1, page_len, 1), 2)
    out_ref[...] = jnp.where(pos < left, fresh_ref[...], cache_ref[...])


def write_cache(kv_cache, fresh, page_table, lengths):
    two, slots, page_len, feat = kv_cache.shape
    page_count = page_table.shape[1]
    hits = page_table[0][None, :] == jnp.arange(slots, dtype=jnp.int32)[:, None]
    pages = jnp.max(jnp.where(hits, jnp.arange(page_count, dtype=jnp.int32)[None], -1), axis=1)
    block = (2, 1, page_len, feat)
    return pl.pallas_call(
        fill_page,
        grid_spec=pltpu.PrefetchScalarGridSpec(
            num_scalar_prefetch=2,
            grid=(slots,),
            in_specs=[
                pl.BlockSpec(block, lambda s, pages, length: (0, s, 0, 0)),
                pl.BlockSpec(block, lambda s, pages, length: (0, jnp.maximum(pages[s], 0), 0, 0)),
            ],
            out_specs=pl.BlockSpec(block, lambda s, pages, length: (0, s, 0, 0)),
        ),
        out_shape=jax.ShapeDtypeStruct(kv_cache.shape, kv_cache.dtype),
        name="fill_pages",
    )(pages, lengths, kv_cache, fresh)


def body(order, tokens, ln_gain, ln_bias, w_qkv, b_qkv, w_out, b_out, kv_cache, page_table,
         lengths):
    n = len(order)
    h = n // 2
    rows, model = tokens.shape
    feat = w_qkv.shape[2]
    total = rows * n
    normed = layer_norm(tokens, ln_gain, ln_bias)
    vmem = pl.BlockSpec(memory_space=pltpu.VMEM)
    anywhere = pl.BlockSpec(memory_space=pl.ANY)
    bf16 = jnp.bfloat16
    attn_out, fresh = pl.pallas_call(
        functools.partial(fused, order),
        out_shape=(
            jax.ShapeDtypeStruct((rows, model), bf16),
            jax.ShapeDtypeStruct((2, total, feat), bf16),
        ),
        in_specs=[vmem, anywhere, vmem, anywhere, vmem, pl.BlockSpec(memory_space=pltpu.SMEM)],
        out_specs=(vmem, anywhere),
        scratch_shapes=[
            pltpu.VMEM((2, total, model // 2), bf16),
            pltpu.VMEM((3, model, feat), bf16),
            pltpu.VMEM((feat, model), bf16),
            pltpu.VMEM((3, total, feat), bf16),
            pltpu.VMEM((2 * rows, feat), bf16),
            pltpu.VMEM((rows, model), bf16),
            pltpu.VMEM((2, h, rows, model), bf16),
            pltpu.SemaphoreType.DMA((2, h + 1, 2)),
            pltpu.SemaphoreType.DMA((2, h + 1, 2)),
            pltpu.SemaphoreType.DMA((2, h + 1, CHUNKS)),
            pltpu.SemaphoreType.DMA((2, h + 1, CHUNKS)),
            pltpu.SemaphoreType.DMA((3,)),
            pltpu.SemaphoreType.DMA,
            pltpu.SemaphoreType.DMA,
        ],
        compiler_params=pltpu.CompilerParams(
            collective_id=0, has_side_effects=True, vmem_limit_bytes=67_043_328
        ),
        name="attention_sublayer",
    )(normed, jnp.transpose(w_qkv, (1, 0, 2)), b_qkv[:, None, :], w_out, b_out[None, :], lengths)
    page_len = kv_cache.shape[2]
    fresh = fresh.reshape(2, total // page_len, page_len, feat)
    return attn_out, write_cache(kv_cache, fresh, page_table, lengths)


def solution(mesh):
    placed = (
        P(("dp", "tp"), None),
        P(),
        P(),
        P(None, None, "tp"),
        P(None, "tp"),
        P("tp", None),
        P(),
        P(None, "dp", None, "tp"),
        P("dp", None),
        P("dp"),
    )
    return jax.shard_map(
        functools.partial(body, ring_order(mesh)),
        mesh=mesh,
        in_specs=placed,
        out_specs=(P(("dp", "tp"), None), P(None, "dp", None, "tp")),
        check_vma=False,
    )
```

time: 381 us -> 187 us (0.49)
  waiting for transfers between devices: 204 us -> 0 us
  Pallas kernels: 0 us -> 178 us
  local copies, waits for them, and re-layouts: 75.4 us -> 1.58 us
  matrix products: 69.8 us -> 0 us
  between operations: 14.8 us -> 1.44 us
  other arithmetic: 12.3 us -> 5.7 us
    pallas_call x0 -> x2, Pallas kernels: none -> 178 us  [the longest x1 171 us: body(): pl.pallas_call(functools.partial(fused, order), out_shape=(jax.ShapeDtype...]
    reduce_scatter x1 -> x0, waiting for transfers between devices: 120 us -> none  [body(): lax.psum_scatter(jnp.dot(attended, w_out, preferred_element_type=jnp.floa...]
    all_gather x1 -> x0, waiting for transfers between devices: 83.8 us -> none  [body(): block_rows = lax.all_gather(normed, 'tp', axis=0, tiled=True)]
    dot_general x7 -> x0, matrix products: 52.6 us -> none  [the longest x1 25.8 us: body(): jnp.dot(block_rows, weights_flat, preferred_element_type=jnp.float32)]
    unnamed x21 -> x11, local copies, waits for them, and re-layouts: 47.6 us -> 0.97 us
    sub x5 -> x0, matrix products: 17.3 us -> none  [one_block(): raised = jnp.exp(scores - row_max)]
    transpose x2 -> x0, local copies, waits for them, and re-layouts: 5.63 us -> none  [write_cache(): jnp.moveaxis(key_value, 1, 0)]
    scatter x1 -> x0, local copies, waits for them, and re-layouts: 4.18 us -> none  [write_cache(): return kv_cache.at[:, slot_ids].set(new_pages)]
  transfers between devices with their start and end apart: 2 -> 0, of which waited for: 2 -> 0; matrix products, arithmetic and copies ran while one was open for 14% -> 0% of each run, Pallas kernels for 0% -> 0%
where the time goes in v1:
time: 187 us; the launch traced here: 186 us
  Pallas kernels  178 us (95%)
  other arithmetic  5.7 us (3%)
    pallas_call x1, Pallas kernels, body(): pl.pallas_call(functools.partial(fused, order), out_shape=(jax.ShapeDtype...  171 us
    pallas_call x1, Pallas kernels, write_cache(): pl.pallas_call(fill_page, grid_spec=pltpu.PrefetchScalarGridSpec(num_scal...  6.95 us

profile of v1, /device:TPU:0, one launch (start us, length us, event | category | flops | bytes accessed | tf_op | source)
XLA Modules:
  0.0 186.4 jit_solution(17537287706379016433)
XLA Ops:
  0.6 0.0 copy-start
  0.6 0.0 copy-start.4
  0.7 0.0 copy-start.2
  0.7 0.0 copy-start.3
  1.4 1.3 select_reduce_fusion.pages_ref
  2.7 1.4 convert_reduce_fusion
  4.1 1.6 fusion.2
  5.8 0.0 copy-done.4
  5.8 0.6 broadcast_in_dim.24.b_ref
  6.4 0.0 copy-done
  6.4 0.0 copy-done.2
  6.4 0.0 copy-done.3
  6.4 1.4 fusion.5.x_ref
  7.8 170.7 %attention_sublayer.1 = (bf16[80,6144]{1,0:T(8,128)(2,1)}, bf16[2,640,768]{2,1,0:T(8,128)(2,1)}) custom-call(bf16[80,6144]{1,0:T(8,128)(2,1)} %fusion.5.x_ref, bf16[3,6144,768]{2,1,0:T(8,128)(2,1)} %bitcast.4, f32[3,1,768]{2,1,0:T(1,128)} %broadcast_in_dim.24.b_ref, bf16[768,6144]{1,0:T(8,128)(2,1)} %wo_hbm.1, f32[1,6144]{1,0:T(1,128)} %bitcast.6, ...), custom_call_target="tpu_custom_call" | custom-call | tf_op jit(solution)/shard_map/attention_sublayer/pallas_call | solution.py:263
  178.5 0.0 copy-start.1
  178.5 7.0 %fill_pages.1 = bf16[2,7,128,768]{3,2,1,0:T(8,128)(2,1)} custom-call(s32[7]{0:T(128)} %select_reduce_fusion.pages_ref, s32[1]{0:T(128)S(6)} %copy.13.len_ref.length_ref, bf16[2,7,128,768]{3,2,1,0:T(8,128)(2,1)} %cache_ref.1, bf16[2,5,128,768]{3,2,1,0:T(8,128)(2,1)} %bitcast.5), custom_call_target="tpu_custom_call" | custom-call | tf_op jit(solution)/shard_map/fill_pages/pallas_call | solution.py:236
  185.5 0.0 copy-done.1
  185.5 0.9 copy.14
  (2 shorter events, 0.0 us)
Async XLA Ops:
  0.6 5.7 %copy-start = (bf16[80,6144]{1,0:T(8,128)(2,1)S(1)}, bf16[80,6144]{1,0:T(8,128)(2,1)}, u32[]{:S(2)}) copy-start(bf16[80,6144]{1,0:T(8,128)(2,1)} %param.10) | copy-start | bytes 2949124
  0.6 5.1 %copy-start.4 = (f32[3,768]{1,0:T(4,128)S(1)}, f32[3,768]{1,0:T(4,128)}, u32[]{:S(2)}) copy-start(f32[3,768]{1,0:T(4,128)} %param.14) | copy-start | bytes 27652
  0.7 5.7 %copy-start.2 = (f32[6144]{0:T(1024)S(1)}, f32[6144]{0:T(1024)}, u32[]{:S(2)}) copy-start(f32[6144]{0:T(1024)} %param.12) | copy-start | bytes 73732
  0.7 5.7 %copy-start.3 = (f32[6144]{0:T(1024)S(1)}, f32[6144]{0:T(1024)}, u32[]{:S(2)}) copy-start(f32[6144]{0:T(1024)} %param.11) | copy-start | bytes 73732
  178.5 7.0 %copy-start.1 = (bf16[80,6144]{1,0:T(8,128)(2,1)S(1)}, bf16[80,6144]{1,0:T(8,128)(2,1)}, u32[]{:S(2)}) copy-start(bf16[80,6144]{1,0:T(8,128)(2,1)} %get-tuple-element.8) | copy-start | bytes 2949124

commit v2 on v1

v2 whole, which is shorter than its diff:
```python
import functools
import math

import jax
import jax.numpy as jnp
import numpy as np
from jax import lax
from jax.experimental import pallas as pl
from jax.experimental.pallas import tpu as pltpu
from jax.sharding import PartitionSpec as P

HD = 128
CHUNKS = 4
PIECES = 4
MESH = pl.DeviceIdType.MESH

norm_eps = 1e-05


def ring_order(mesh):
    n = mesh.shape["tp"]
    line = np.moveaxis(mesh.devices, mesh.axis_names.index("tp"), -1).reshape(-1, n)[0]
    coords = [tuple(getattr(d, "coords", None) or ()) for d in line]
    wide = len({c[0] for c in coords if c})
    if wide < 2 or n % wide or (n // wide) % 2:
        return list(range(n))
    tall = n // wide
    order = [0]
    for z in range(tall):
        xs = range(1, wide) if z % 2 == 0 else range(wide - 1, 0, -1)
        order += [z * wide + x for x in xs]
    order += [z * wide for z in range(tall - 1, 0, -1)]
    return order


def pick(table, index):
    value = jnp.int32(0)
    for k, entry in enumerate(table):
        value = value + jnp.where(index == k, entry, 0)
    return value


def fused(order, x_hbm, gain_ref, shift_ref, w_hbm, b_ref, wo_hbm, bo_ref, cache_hbm, table_ref,
          len_ref, out_ref, kv_hbm,
          xg, w_v, wo_v, proj, att, first, rs, held, bias,
          ag_send, ag_recv, tail_send, tail_recv, rs_send, rs_recv,
          x_sem, w_sem, wo_sem, in_sem, kv_sem):
    n = len(order)
    h = n // 2
    rows, model = x_hbm.shape
    mid = model // 2
    feat = w_v.shape[2]
    total = proj.shape[1]
    me = lax.axis_index("tp")
    inverse = [order.index(i) for i in range(n)]
    place = pick(inverse, me)

    def at(offset):
        return pick(order, lax.rem(place + offset + n, n))

    peers = (at(1), at(-1))
    x_copy = pltpu.make_async_copy(x_hbm, first, x_sem)
    x_copy.start()
    barrier = pltpu.get_barrier_semaphore()
    for peer in peers:
        pl.semaphore_signal(barrier, inc=1, device_id={"tp": peer}, device_id_type=MESH)
    x_copy.wait()
    for c in range(3):
        pltpu.make_async_copy(w_hbm.at[c], w_v.at[c], w_sem.at[c]).start()
    wo_copy = pltpu.make_async_copy(wo_hbm, wo_v, wo_sem)
    wo_copy.start()

    for c in range(3):
        bias[c] = b_ref[pl.ds(c, 1), :]
    group = math.gcd(rows, 16)

    @pl.loop(0, rows // group)
    def _(i):
        part = pl.ds(pl.multiple_of(i * group, group), group)
        floats = first[part, :].astype(jnp.float32)
        center = jnp.mean(floats, axis=-1, keepdims=True)
        spread = jnp.mean(jnp.square(floats - center), axis=-1, keepdims=True)
        normed = ((floats - center) * lax.rsqrt(spread + norm_eps) * gain_ref[...]
                  + shift_ref[...]).astype(jnp.bfloat16)
        xg[0, part, :] = normed[:, :mid]
        xg[1, part, :] = normed[:, mid:]

    pl.semaphore_wait(barrier, 2)

    def slot(way, s):
        return 0 if s == 0 else n - 1 if s == h else 2 * s - 1 + way

    def gather(way, s, half):
        return pltpu.make_async_remote_copy(
            src_ref=xg.at[half, pl.ds(slot(way, s - 1) * rows, rows)],
            dst_ref=xg.at[half, pl.ds(slot(way, s) * rows, rows)],
            send_sem=ag_send.at[way, s, half], recv_sem=ag_recv.at[way, s, half],
            device_id={"tp": peers[way]}, device_id_type=MESH)

    piece = mid // PIECES

    def tail(way, e):
        cols = pl.ds(e * piece, piece)
        return pltpu.make_async_remote_copy(
            src_ref=xg.at[way, pl.ds(slot(way, h - 1) * rows, rows), cols],
            dst_ref=xg.at[way, pl.ds((n - 1) * rows, rows), cols],
            send_sem=tail_send.at[way, e], recv_sem=tail_recv.at[way, e],
            device_id={"tp": peers[way]}, device_id_type=MESH)

    gathers = [(way, s, k if way == 0 else 1 - k)
               for s in range(1, h) for k in range(2) for way in range(2)]
    for g in gathers:
        if g[1] == 1:
            gather(*g).start()
    for c in range(3):
        pltpu.make_async_copy(w_hbm.at[c], w_v.at[c], w_sem.at[c]).wait()

    tn = math.gcd(feat, 256)

    def project(lhs, owners):
        @pl.loop(0, 3)
        def _(c):
            @pl.loop(0, feat // tn)
            def _(j):
                cols = pl.ds(pl.multiple_of(j * tn, tn), tn)
                acc = jnp.dot(lhs(0), w_v[c, pl.ds(0, mid), cols],
                              preferred_element_type=jnp.float32)
                acc += jnp.dot(lhs(1), w_v[c, pl.ds(mid, mid), cols],
                               preferred_element_type=jnp.float32)
                done = (acc + bias[c, :, cols]).astype(jnp.bfloat16)
                for i, owner in enumerate(owners):
                    dst = pl.ds(pl.multiple_of(owner * rows, rows), rows)
                    proj[c, dst, cols] = done[i * rows:(i + 1) * rows]

    def project_tail(e):
        far = pl.ds((n - 1) * rows, rows)
        here = pl.ds(e * piece, piece)

        @pl.loop(0, 3)
        def _(c):
            @pl.loop(0, feat // tn)
            def _(j):
                cols = pl.ds(pl.multiple_of(j * tn, tn), tn)
                acc = jnp.dot(xg[0, far, here], w_v[c, here, cols],
                              preferred_element_type=jnp.float32)
                acc += jnp.dot(xg[1, far, here], w_v[c, pl.ds(mid + e * piece, piece), cols],
                               preferred_element_type=jnp.float32)
                if e > 0:
                    acc += held[c, :, cols]
                if e < PIECES - 1:
                    held[c, :, cols] = acc
                else:
                    dst = pl.ds(pl.multiple_of(at(h) * rows, rows), rows)
                    proj[c, dst, cols] = (acc + bias[c, :, cols]).astype(jnp.bfloat16)

    project(lambda half: xg[half, pl.ds(0, rows)], [me])
    for s in range(1, h):
        for g in gathers:
            if g[1] == s:
                way, _, half = g
                gather(*g).wait_recv()
                if s + 1 < h:
                    gather(way, s + 1, half).start()
                elif half == way:
                    for e in range(PIECES):
                        tail(way, e).start()
        project(lambda half: xg[half, pl.ds((2 * s - 1) * rows, 2 * rows)], [at(-s), at(s)])
    for e in range(PIECES):
        for way in range(2):
            tail(way, e).wait_recv()
        project_tail(e)

    slots, page_len = cache_hbm.shape[1:3]

    def page(i, s):
        return w_v.at[i, pl.ds(s * page_len, page_len)]

    def cache_in(i, s):
        return pltpu.make_async_copy(cache_hbm.at[i, s], page(i, s), in_sem.at[i, s])

    def cache_out(i, s):
        return pltpu.make_async_copy(page(i, s), kv_hbm.at[i, s], kv_sem.at[i, s])

    pages = [(i, s) for i in range(2) for s in range(slots)]
    length = len_ref[0]

    def fill_pages():
        for i, s in pages:
            cache_in(i, s).wait()
        pos = lax.broadcasted_iota(jnp.int32, (page_len, feat), 0)

        @pl.loop(0, slots)
        def _(s):
            here = pl.ds(pl.multiple_of(s * page_len, page_len), page_len)
            for i in range(2):
                held_page = w_v[i, here, :]
                for k in range(table_ref.shape[1]):
                    left = jnp.where(table_ref[0, k] == s, length - k * page_len, 0)
                    held_page = jnp.where(
                        pos < left, proj[i + 1, pl.ds(k * page_len, page_len), :], held_page)
                w_v[i, here, :] = held_page

        for i, s in pages:
            cache_out(i, s).start()

    scale = 1.0 / math.sqrt(HD)

    def attend(owners):
        key_pos = lax.broadcasted_iota(jnp.int32, (rows, total), 1)
        row_pos = lax.broadcasted_iota(jnp.int32, (rows, total), 0)

        heads = feat // HD
        per = 1 if len(owners) > 1 else math.gcd(heads, 3)

        @pl.loop(0, heads // per)
        def _(turn):
            for i, b in [(i, b) for i in range(per) for b in range(len(owners))]:
                owner = owners[b]
                cols = pl.ds(pl.multiple_of((turn * per + i) * HD, HD), HD)
                query = proj[0, pl.ds(pl.multiple_of(owner * rows, rows), rows), cols]
                scores = lax.dot_general(query, proj[1, :, cols], (((1,), (1,)), ((), ())),
                                         preferred_element_type=jnp.float32) * scale
                allowed = (key_pos <= row_pos + owner * rows) & (key_pos < length)
                scores = jnp.where(allowed, scores, -1e30)
                raised = jnp.exp(scores - jnp.max(scores, axis=-1, keepdims=True))
                share = 1.0 / jnp.sum(raised, axis=-1, keepdims=True)
                att[pl.ds(b * rows, rows), cols] = jnp.dot(
                    (raised * share).astype(jnp.bfloat16), proj[2, :, cols],
                    preferred_element_type=jnp.float32).astype(jnp.bfloat16)

    chunk = model // CHUNKS
    to = math.gcd(chunk, 512)

    def scatter(way, d, q):
        cols = pl.ds(q * chunk, chunk)
        src = first.at[:, cols] if d == h else rs.at[way, d, :, cols]
        return pltpu.make_async_remote_copy(
            src_ref=src, dst_ref=rs.at[way, d - 1, :, cols],
            send_sem=rs_send.at[way, d, q], recv_sem=rs_recv.at[way, d, q],
            device_id={"tp": peers[way]}, device_id_type=MESH)

    scatters = [(way, d, q) for d in range(h, 0, -1) for q in range(CHUNKS) for way in range(2)
                if d < h or way == q // (CHUNKS // 2)]

    wo_copy.wait()
    attend([at(h)])
    half = CHUNKS // 2
    turns = [0, half] + [c for c in range(CHUNKS) if c not in (0, half)]
    for q in turns:
        @pl.loop(0, chunk // to)
        def _(j):
            cols = pl.ds(pl.multiple_of(q * chunk + j * to, to), to)
            first[:, cols] = jnp.dot(att[pl.ds(0, rows), :], wo_v[:, cols],
                                     preferred_element_type=jnp.float32).astype(jnp.bfloat16)
        for way in range(2):
            if (way, h, q) in scatters:
                scatter(way, h, q).start()

    for i, s in pages:
        cache_in(i, s).start()

    for d in range(h - 1, 0, -1):
        attend([at(d), at(-d)])
        for q in turns:
            have = [(way, d + 1, q) in scatters for way in range(2)]
            for way in range(2):
                if have[way]:
                    scatter(way, d + 1, q).wait_recv()

            @pl.loop(0, chunk // to)
            def _(j):
                cols = pl.ds(pl.multiple_of(q * chunk + j * to, to), to)
                part = jnp.dot(att[...], wo_v[:, cols], preferred_element_type=jnp.float32)
                for way in range(2):
                    mine = part[way * rows:(way + 1) * rows]
                    if have[way]:
                        mine = mine + rs[way, d, :, cols].astype(jnp.float32)
                    rs[way, d, :, cols] = mine.astype(jnp.bfloat16)
            for way in range(2):
                scatter(way, d, q).start()
        if d == h - 1:
            fill_pages()

    attend([me])
    for q in turns:
        for way in range(2):
            scatter(way, 1, q).wait_recv()

        @pl.loop(0, chunk // to)
        def _(j):
            cols = pl.ds(pl.multiple_of(q * chunk + j * to, to), to)
            part = jnp.dot(att[pl.ds(0, rows), :], wo_v[:, cols],
                           preferred_element_type=jnp.float32)
            part += rs[0, 0, :, cols].astype(jnp.float32) + rs[1, 0, :, cols].astype(jnp.float32)
            out_ref[:, cols] = (part + bo_ref[:, cols]).astype(jnp.bfloat16)

    for g in gathers:
        gather(*g).wait_send()
    for e in range(PIECES):
        for way in range(2):
            tail(way, e).wait_send()
    for g in scatters:
        scatter(*g).wait_send()
    for i, s in pages:
        cache_out(i, s).wait()


def body(order, tokens, ln_gain, ln_bias, w_qkv, b_qkv, w_out, b_out, kv_cache, page_table,
         lengths):
    n = len(order)
    h = n // 2
    rows, model = tokens.shape
    feat = w_qkv.shape[2]
    total = rows * n
    vmem = pl.BlockSpec(memory_space=pltpu.VMEM)
    anywhere = pl.BlockSpec(memory_space=pl.ANY)
    bf16 = jnp.bfloat16
    smem = pl.BlockSpec(memory_space=pltpu.SMEM)
    slots = kv_cache.shape[1]
    dma = pltpu.SemaphoreType.DMA
    return pl.pallas_call(
        functools.partial(fused, order),
        out_shape=(
            jax.ShapeDtypeStruct((rows, model), bf16),
            jax.ShapeDtypeStruct(kv_cache.shape, bf16),
        ),
        in_specs=[anywhere, vmem, vmem, anywhere, vmem, anywhere, vmem, anywhere, smem, smem],
        out_specs=(vmem, anywhere),
        scratch_shapes=[
            pltpu.VMEM((2, total, model // 2), bf16),
            pltpu.VMEM((3, model, feat), bf16),
            pltpu.VMEM((feat, model), bf16),
            pltpu.VMEM((3, total, feat), bf16),
            pltpu.VMEM((2 * rows, feat), bf16),
            pltpu.VMEM((rows, model), bf16),
            pltpu.VMEM((2, h, rows, model), bf16),
            pltpu.VMEM((3, rows, feat), jnp.float32),
            pltpu.VMEM((3, 1, feat), jnp.float32),
            dma((2, h, 2)),
            dma((2, h, 2)),
            dma((2, PIECES)),
            dma((2, PIECES)),
            dma((2, h + 1, CHUNKS)),
            dma((2, h + 1, CHUNKS)),
            dma,
            dma((3,)),
            dma,
            dma((2, slots)),
            dma((2, slots)),
        ],
        compiler_params=pltpu.CompilerParams(
            collective_id=0, has_side_effects=True, vmem_limit_bytes=67_043_328
        ),
        name="attention_sublayer",
    )(tokens, ln_gain[None, :], ln_bias[None, :], jnp.transpose(w_qkv, (1, 0, 2)), b_qkv, w_out,
      b_out[None, :], kv_cache, page_table, lengths)


def solution(mesh):
    placed = (
        P(("dp", "tp"), None),
        P(),
        P(),
        P(None, None, "tp"),
        P(None, "tp"),
        P("tp", None),
        P(),
        P(None, "dp", None, "tp"),
        P("dp", None),
        P("dp"),
    )
    return jax.shard_map(
        functools.partial(body, ring_order(mesh)),
        mesh=mesh,
        in_specs=placed,
        out_specs=(P(("dp", "tp"), None), P(None, "dp", None, "tp")),
        check_vma=False,
    )
```

time: 187 us -> 177 us (0.947)
  Pallas kernels: 178 us -> 170 us
  other arithmetic: 5.7 us -> 0 us
  local copies, waits for them, and re-layouts: 1.58 us -> 5.72 us
    pallas_call x1 -> x0, Pallas kernels: 6.95 us -> none  [write_cache(): pl.pallas_call(fill_page, grid_spec=pltpu.PrefetchScalarGridSpec(num_scal...]
    unnamed x11 -> x2, local copies, waits for them, and re-layouts: 0.97 us -> 5.72 us
    reduce_sum x2 -> x0, other arithmetic: 3.05 us -> none  [the longest x1 1.62 us: layer_norm(): spread = jnp.mean(jnp.square(floats - center), axis=-1, keepdims=True)]
where the time goes in v2:
time: 177 us
  Pallas kernels  170 us (96%)
  local copies, waits for them, and re-layouts  5.72 us (3%)
    pallas_call x1, Pallas kernels, body(): pl.pallas_call(functools.partial(fused, order), out_shape=(jax.ShapeDtype...  170 us
    unnamed x2, local copies, waits for them, and re-layouts  5.72 us

profile of v2, /device:TPU:0, one launch (start us, length us, event | category | flops | bytes accessed | tf_op | source)
XLA Modules:
  0.0 176.9 jit_solution(15335894491655238657)
XLA Ops:
  1.3 169.9 %attention_sublayer.1 = (bf16[80,6144]{1,0:T(8,128)(2,1)}, bf16[2,7,128,768]{3,2,1,0:T(8,128)(2,1)}) custom-call(bf16[80,6144]{1,0:T(8,128)(2,1)} %x_hbm.1, f32[1,6144]{1,0:T(1,128)} %bitcast.5, f32[1,6144]{1,0:T(1,128)} %bitcast.6, bf16[3,6144,768]{2,1,0:T(8,128)(2,1)} %bitcast.4, f32[3,768]{1,0:T(4,128)} %b_ref.1, bf16[768,6144]{1,0:T(8,128)(2,1)} %wo_hbm.1, ...), custom_call_target="tpu_custom_call" | custom-call | tf_op jit(solution)/shard_map/attention_sublayer/pallas_call | solution.py:321
  171.2 2.2 %copy.15 = bf16[80,6144]{1,0:T(8,128)(2,1)} copy(bf16[80,6144]{1,0:T(8,128)(2,1)} %get-tuple-element.4) | data formatting | bytes 1966080
  173.4 3.5 %copy.16 = bf16[2,7,128,768]{3,2,1,0:T(8,128)(2,1)} copy(bf16[2,7,128,768]{3,2,1,0:T(8,128)(2,1)} %get-tuple-element.5) | data formatting | bytes 5505024

commit v3 on v2

--- a/solution.py
+++ b/solution.py
@@ -115,7 +115,7 @@
     for c in range(3):
         pltpu.make_async_copy(w_hbm.at[c], w_v.at[c], w_sem.at[c]).wait()
 
-    tn = math.gcd(feat, 256)
+    tn = math.gcd(feat, 768)
 
     def project(lhs, owners):
         @pl.loop(0, 3)
@@ -133,7 +133,8 @@
                     proj[c, dst, cols] = done[i * rows:(i + 1) * rows]
 
     def project_tail(e):
-        far = pl.ds((n - 1) * rows, rows)
+        far = pl.ds((n - 3) * rows, 3 * rows)
+        owners = [at(1 - h), at(h - 1), at(h)]
         here = pl.ds(e * piece, piece)
 
         @pl.loop(0, 3)
@@ -150,8 +151,10 @@
                 if e < PIECES - 1:
                     held[c, :, cols] = acc
                 else:
-                    dst = pl.ds(pl.multiple_of(at(h) * rows, rows), rows)
-                    proj[c, dst, cols] = (acc + bias[c, :, cols]).astype(jnp.bfloat16)
+                    done = (acc + bias[c, :, cols]).astype(jnp.bfloat16)
+                    for i, owner in enumerate(owners):
+                        dst = pl.ds(pl.multiple_of(owner * rows, rows), rows)
+                        proj[c, dst, cols] = done[i * rows:(i + 1) * rows]
 
     project(lambda half: xg[half, pl.ds(0, rows)], [me])
     for s in range(1, h):
@@ -164,7 +167,8 @@
                 elif half == way:
                     for e in range(PIECES):
                         tail(way, e).start()
-        project(lambda half: xg[half, pl.ds((2 * s - 1) * rows, 2 * rows)], [at(-s), at(s)])
+        if s < h - 1:
+            project(lambda half: xg[half, pl.ds((2 * s - 1) * rows, 2 * rows)], [at(-s), at(s)])
     for e in range(PIECES):
         for way in range(2):
             tail(way, e).wait_recv()
@@ -229,7 +233,7 @@
                     preferred_element_type=jnp.float32).astype(jnp.bfloat16)
 
     chunk = model // CHUNKS
-    to = math.gcd(chunk, 512)
+    to = math.gcd(chunk, 768)
 
     def scatter(way, d, q):
         cols = pl.ds(q * chunk, chunk)
@@ -334,7 +338,7 @@
             pltpu.VMEM((2 * rows, feat), bf16),
             pltpu.VMEM((rows, model), bf16),
             pltpu.VMEM((2, h, rows, model), bf16),
-            pltpu.VMEM((3, rows, feat), jnp.float32),
+            pltpu.VMEM((3, 3 * rows, feat), jnp.float32),
             pltpu.VMEM((3, 1, feat), jnp.float32),
             dma((2, h, 2)),
             dma((2, h, 2)),

time: 177 us -> 173 us (0.977)
  Pallas kernels: 170 us -> 166 us
    pallas_call x1, Pallas kernels: 170 us -> 166 us  [body(): pl.pallas_call(functools.partial(fused, order), out_shape=(jax.ShapeDtype...]
where the time goes in v3:
time: 173 us
  Pallas kernels  166 us (96%)
  local copies, waits for them, and re-layouts  5.72 us (3%)
    pallas_call x1, Pallas kernels, body(): pl.pallas_call(functools.partial(fused, order), out_shape=(jax.ShapeDtype...  166 us
    unnamed x2, local copies, waits for them, and re-layouts  5.72 us

profile of v3, /device:TPU:0, one launch (start us, length us, event | category | flops | bytes accessed | tf_op | source)
XLA Modules:
  0.0 173.1 jit_solution(2186135423497521792)
XLA Ops:
  1.3 166.1 %attention_sublayer.1 = (bf16[80,6144]{1,0:T(8,128)(2,1)}, bf16[2,7,128,768]{3,2,1,0:T(8,128)(2,1)}) custom-call(bf16[80,6144]{1,0:T(8,128)(2,1)} %x_hbm.1, f32[1,6144]{1,0:T(1,128)} %bitcast.5, f32[1,6144]{1,0:T(1,128)} %bitcast.6, bf16[3,6144,768]{2,1,0:T(8,128)(2,1)} %bitcast.4, f32[3,768]{1,0:T(4,128)} %b_ref.1, bf16[768,6144]{1,0:T(8,128)(2,1)} %wo_hbm.1, ...), custom_call_target="tpu_custom_call" | custom-call | tf_op jit(solution)/shard_map/attention_sublayer/pallas_call | solution.py:325
  167.4 2.2 %copy.15 = bf16[80,6144]{1,0:T(8,128)(2,1)} copy(bf16[80,6144]{1,0:T(8,128)(2,1)} %get-tuple-element.4) | data formatting | bytes 1966080
  169.6 3.5 %copy.16 = bf16[2,7,128,768]{3,2,1,0:T(8,128)(2,1)} copy(bf16[2,7,128,768]{3,2,1,0:T(8,128)(2,1)} %get-tuple-element.5) | data formatting | bytes 5505024
